TPU v7x, 256 devices: a whole 4x4x8 slice. The times are simulated.
256 devices in a mesh: blk: 128 (over z_lo, y, x, core), rep: 2 (over z_hi).
Axes of the slice: x: 4, y: 4, z: 8 (z_hi: 2, z_lo: 4; z = z_hi * 4 + z_lo), core: 2. Of those that a mesh axis runs over, the one named last changes fastest.
Arguments:
- load_coef: bfloat16 [256, 2049, 256], P('blk', None, 'rep'), parts along dimension 2, may hold values from -0.29882812 to 0.29882812
- legendre: bfloat16 [256, 2049, 1024], P('blk'), may hold values from -0.125 to 0.125
- slab_orders: int32 [256], replicated, may hold values from 0 to 1023, as said below
- cycle_rows: int32 [1024], replicated, may hold values from 0 to 1023, each once
Outputs:
- potential: bfloat16 [1024, 128, 4096], P('blk', 'rep'), parts along dimension 1
- energy: float32 [128], P('rep'), parts along dimension 0
There are 2 independent parts, one for each index of `rep`. A program takes and returns all parts, laid end to end along the dimension named above; an argument that names none is the same for every part. Nothing has to cross between parts.
Inputs may be any that keep to these rules, and one draw needn't show every extreme that they name: `slab_orders`: values are distinct and below (2048) / 2. `cycle_rows`: each cycle appears once.
All inputs are finite; a program needn't handle non-finite values.
Results may differ from a plain program's by a relative error of at most 0.0055.
Values may be sent and summed in bfloat16 or wider, within the bound.
No kernel may reach another device: no remote copies, remote signals or barrier semaphores. Data moves between devices by JAX's collectives and lax.ppermute only.
A program may use at most 128 MiB of HBM per device.

v0:
```python
import math
import jax
import jax.numpy as jnp
from jax import lax
from jax.sharding import Mesh
from jax.sharding import PartitionSpec as P

NLON = 4096
BLK = ("blk_0", "blk_1", "blk_2", "blk_3")


def one_axis_at_a_time(x, axes):
    for axis in axes:
        x = lax.psum(x, axis)
    return x


def basis_rows(frequency):
    coarse_ids = jnp.arange(NLON // 64, dtype=jnp.int32) * 64
    fine_ids = jnp.arange(64, dtype=jnp.int32)
    scale = 2.0 * math.pi / NLON
    coarse_angles = (frequency[:, None] * coarse_ids[None, :] % NLON).astype(jnp.float32) * scale
    fine_angles = (frequency[:, None] * fine_ids[None, :] % NLON).astype(jnp.float32) * scale
    cos_coarse = jnp.cos(coarse_angles)[:, :, None]
    sin_coarse = jnp.sin(coarse_angles)[:, :, None]
    cos_fine = jnp.cos(fine_angles)[:, None, :]
    sin_fine = jnp.sin(fine_angles)[:, None, :]
    cosine = (cos_coarse * cos_fine - sin_coarse * sin_fine).reshape(frequency.shape[0], NLON)
    sine = (sin_coarse * cos_fine + cos_coarse * sin_fine).reshape(frequency.shape[0], NLON)
    factor = jnp.where(frequency == 0, 1.0, 2.0).astype(jnp.float32)[:, None]
    return ((factor * cosine).astype(jnp.bfloat16), (-factor * sine).astype(jnp.bfloat16))


def fourier(received, low_orders, degree):
    cos_lower, sin_lower = basis_rows(low_orders)
    cos_upper, sin_upper = basis_rows(degree - low_orders)
    fourier_basis = jnp.stack([cos_lower, sin_lower, cos_upper, sin_upper], axis=1)
    return jnp.einsum("rnsf,nsk->rfk", received, fourier_basis, preferred_element_type=jnp.float32)


def shards(load_coef, legendre, slab_orders, cycle_rows):
    blocks = lax.axis_size(BLK)
    position = lax.axis_index(BLK)
    pair_count = load_coef.shape[0]
    slab_rows = load_coef.shape[1]
    fields = load_coef.shape[2] // 2
    lat_count = legendre.shape[2]
    degree = slab_rows - 2
    my_orders = lax.dynamic_slice_in_dim(slab_orders, position * pair_count, pair_count)
    row_ids = jnp.arange(slab_rows, dtype=jnp.int32)
    spectra = []
    for pair_index in range(pair_count):
        in_lower = (row_ids < slab_rows - 1 - my_orders[pair_index])[:, None]
        pair_coef = load_coef[pair_index]
        nothing = jnp.zeros_like(pair_coef)
        stacked = jnp.concatenate(
            [jnp.where(in_lower, pair_coef, nothing), jnp.where(in_lower, nothing, pair_coef)],
            axis=1,
        )
        spectra.append(
            lax.dot_general(
                legendre[pair_index],
                stacked,
                (((0,), (0,)), ((), ())),
                preferred_element_type=jnp.float32,
            ).astype(jnp.bfloat16)
        )
    spectra = jnp.stack(spectra, axis=1).reshape(lat_count, pair_count, 4, fields)
    spectra = jnp.take(spectra, cycle_rows, axis=0)
    all_orders = slab_orders.reshape(blocks, pair_count)
    cycle_grid = fourier(
        lax.all_to_all(spectra, BLK, split_axis=0, concat_axis=1, tiled=True),
        low_orders=all_orders.reshape(-1),
        degree=degree,
    )
    partial_energy = jnp.sum(cycle_grid * cycle_grid, axis=(0, 2))
    summed = one_axis_at_a_time(partial_energy, BLK)
    energy = summed / (lat_count * NLON)
    return (cycle_grid.astype(jnp.bfloat16), energy)


def solution(mesh):
    split = Mesh(
        mesh.devices.reshape(4, 4, 4, 2, mesh.shape["rep"]),
        ("blk_0", "blk_1", "blk_2", "blk_3", "rep"),
    )
    in_specs = (P(BLK, None, "rep"), P(BLK, None, None), P(), P())
    out_specs = (P(BLK, "rep", None), P("rep"))
    return jax.shard_map(
        shards, mesh=split, in_specs=in_specs, out_specs=out_specs, check_vma=False
    )
```

profile of v0, /device:TPU:1, one launch (start us, length us, event | category | flops | bytes accessed | tf_op | source)
XLA Modules:
  0.0 158.2 jit_solution(1284161723024664103)
XLA Ops:
  4.7 3.6 %fusion.52 = (bf16[1,2049,128]{2,0,1:T(2,128)(2,1)S(1)}, bf16[1,2049,128]{2,0,1:T(2,128)(2,1)S(1)}) fusion(bf16[2,2049,128]{2,0,1:T(2,128)(2,1)} %param.4), kind=kLoop, calls=%fused_computation.100 | loop fusion | bytes 2098176 | tf_op jit(solution)/shard_map/slice | solution.py:54
  8.3 17.4 %fusion.51 = (bf16[1,2049,1024]{2,0,1:T(2,128)(2,1)S(1)}, bf16[1,2049,1024]{2,0,1:T(2,128)(2,1)}) fusion(bf16[2,2049,1024]{2,0,1:T(2,128)(2,1)} %param.5), kind=kLoop, calls=%fused_computation.99 | loop fusion | bytes 16785408 | tf_op jit(solution)/shard_map/slice | solution.py:62
  25.7 1.9 %broadcast_select_fusion.2 = (bf16[2049,128]{1,0:T(8,128)(2,1)S(1)}, bf16[2049,128]{1,0:T(8,128)(2,1)S(1)}, bf16[2049,128]{1,0:T(8,128)(2,1)S(1)}, bf16[2049,128]{1,0:T(8,128)(2,1)S(1)}) fusion(pred[2049]{0:T(1024)(128)(4,1)S(1)} %iota_compare_fusion, bf16[1,2049,128]{2,0,1:T(2,128)(2,1)S(1)} %get-tuple-element.9, ...), kind=kLoop, calls=%fused_computation.39 | loop fusion | flops 1049088 | bytes 3151362 | tf_op jit(solution)/shard_map/jit(_where)/select_n | solution.py:57
  27.7 1.5 fusion.11
  29.9 4.9 %fusion.12 = bf16[256,1024]{1,0:T(8,128)(2,1)S(1)} fusion(bf16[1,2049,1024]{2,0,1:T(2,128)(2,1)} %get-tuple-element.3, bf16[2049,128]{1,0:T(8,128)(2,1)S(1)} %get-tuple-element.7, bf16[2049,128]{1,0:T(8,128)(2,1)S(1)} %get-tuple-element.6), kind=kOutput, calls=%fused_computation.29 | convolution fusion | flops 1076626432 | bytes 5769728 | tf_op jit(solution)/shard_map/dot_general | solution.py:61
  35.6 3.1 %pad_maximum_fusion = bf16[1024,2,4,64]{3,2,1,0:T(4,128)(2,1)} fusion(bf16[1024,1,4,64]{3,2,1,0:T(4,128)(2,1)S(1)} %copy.13, bf16[1024,1,4,64]{3,2,1,0:T(4,128)(2,1)S(1)} %copy.12), kind=kLoop, calls=%fused_computation.24 | loop fusion | flops 524288 | bytes 2097152 | tf_op jit(solution)/shard_map/stack | solution.py:68
  38.6 5.8 %gather_fusion = bf16[1024,2,4,64]{3,2,1,0:T(4,128)(2,1)S(1)} fusion(bf16[1024,2,4,64]{3,2,1,0:T(4,128)(2,1)} %pad_maximum_fusion, s32[1024]{0:T(1024)S(1)} %fusion.45), kind=kCustom, calls=%fused_computation | custom fusion | bytes 2101248 | tf_op jit(solution)/shard_map/jit(_take)/gather | solution.py:69
  44.5 4.5 %broadcast_select_fusion = bf16[1024,2,4,64]{3,2,1,0:T(4,128)(2,1)} fusion(bf16[1024,2,4,64]{3,2,1,0:T(4,128)(2,1)S(1)} %gather_fusion, pred[1024]{0:T(1024)(128)(4,1)S(1)} %compare_and_fusion), kind=kLoop, calls=%fused_computation.27 | loop fusion | flops 524288 | bytes 2098176 | tf_op jit(solution)/shard_map/jit(_take)/select_n | solution.py:69
  49.0 5.1 %reshape.541 = bf16[128,2,2048]{2,1,0:T(2,128)(2,1)} reshape(bf16[1024,2,4,64]{3,2,1,0:T(4,128)(2,1)} %broadcast_select_fusion) | data formatting | bytes 2097152
  54.0 13.8 %all-to-all-start = ((bf16[128,2,2048]{2,1,0:T(2,128)(2,1)}), bf16[128,2,2048]{2,1,0:T(2,128)(2,1)S(1)}, u32[]{:S(2)}, u32[]{:S(2)}) async-start(bf16[128,2,2048]{2,1,0:T(2,128)(2,1)} %reshape.541), calls=%async_computation | async-start | bytes 2097152 | tf_op jit(solution)/shard_map/all_to_all | solution.py:72
  69.0 6.5 %multiply_subtract_fusion = (f32[256,64,64]{0,2,1:T(8,128)}, f32[256,64,64]{0,2,1:T(8,128)}, f32[256,64,64]{0,2,1:T(8,128)}, f32[256,64,64]{0,2,1:T(8,128)}) fusion(f32[256,64]{0,1:T(8,128)S(1)} %get-tuple-element.29, f32[256,64]{0,1:T(8,128)S(1)} %get-tuple-element.30, f32[256,64]{0,1:T(8,128)S(1)} %get-tuple-element.28, ...), kind=kLoop, calls=%fused_computation.19 | loop fusion | flops 12582912 | bytes 17301504 | tf_op jit(solution)/shard_map/sub | solution.py:28
  75.5 5.6 %copy.19 = f32[256,1,4096]{2,0,1:T(8,128)} copy(f32[256,1,4096]{0,2,1:T(8,128)} %bitcast.54) | data formatting | bytes 8388608 | tf_op jit(solution)/shard_map/add | solution.py:29
  81.1 5.6 %copy.18 = f32[256,1,4096]{2,0,1:T(8,128)} copy(f32[256,1,4096]{0,2,1:T(8,128)} %bitcast.53) | data formatting | bytes 8388608 | tf_op jit(solution)/shard_map/sub | solution.py:28
  86.7 5.6 %copy.17 = f32[256,1,4096]{2,0,1:T(8,128)} copy(f32[256,1,4096]{0,2,1:T(8,128)} %bitcast.52) | data formatting | bytes 8388608 | tf_op jit(solution)/shard_map/add | solution.py:29
  92.3 5.6 %copy.16 = f32[256,1,4096]{2,0,1:T(8,128)} copy(f32[256,1,4096]{0,2,1:T(8,128)} %bitcast.51) | data formatting | bytes 8388608 | tf_op jit(solution)/shard_map/sub | solution.py:28
  97.9 4.1 %multiply_convert_fusion = bf16[256,1,4096]{2,0,1:T(8,128)(2,1)} fusion(f32[256,1,4096]{2,0,1:T(8,128)} %copy.19, f32[256]{0:T(256)S(1)} %get-tuple-element.19), kind=kLoop, calls=%fused_computation.16 | loop fusion | flops 2097152 | bytes 6292480 | tf_op jit(solution)/shard_map/convert_element_type | solution.py:31
  102.1 1.8 %multiply_convert_fusion.1 = bf16[256,1,4096]{2,0,1:T(8,128)(2,1)} fusion(f32[256,1,4096]{2,0,1:T(8,128)S(1)} %copy-done.2, f32[256]{0:T(256)S(1)} %get-tuple-element.21), kind=kLoop, calls=%fused_computation.18 | loop fusion | flops 2097152 | bytes 6292480 | tf_op jit(solution)/shard_map/convert_element_type | solution.py:31
  105.0 1.8 %multiply_convert_fusion.2 = bf16[256,1,4096]{2,0,1:T(8,128)(2,1)} fusion(f32[256,1,4096]{2,0,1:T(8,128)S(1)} %copy-done.1, f32[256]{0:T(256)S(1)} %get-tuple-element.20), kind=kLoop, calls=%fused_computation.20 | loop fusion | flops 2097152 | bytes 6292480 | tf_op jit(solution)/shard_map/convert_element_type | solution.py:31
  106.8 1.8 %multiply_convert_fusion.3 = bf16[256,1,4096]{2,0,1:T(8,128)(2,1)} fusion(f32[256,1,4096]{2,0,1:T(8,128)S(1)} %copy-done, f32[256]{0:T(256)S(1)} %get-tuple-element.18), kind=kLoop, calls=%fused_computation.22 | loop fusion | flops 2097152 | bytes 6292480 | tf_op jit(solution)/shard_map/convert_element_type | solution.py:31
  113.4 7.7 %bitcast_convert_fusion = (bf16[8,64,4096]{2,1,0:T(8,128)(2,1)}, f32[8,64,4096,1]{2,1,3,0:T(8,128)S(1)}) fusion(bf16[256,1,4096]{2,0,1:T(8,128)(2,1)S(1)} %copy-done.3, bf16[256,1,4096]{2,0,1:T(8,128)(2,1)S(1)} %copy-done.4, bf16[256,1,4096]{2,0,1:T(8,128)(2,1)S(1)} %copy-done.5, bf16[256,1,4096]{2,0,1:T(8,128)(2,1)S(1)} %copy-done.6, ...), kind=kOutput, calls=%fused_computation.10 | convolution fusion | flops 4309647360 | bytes 22020096 | tf_op jit(solution)/shard_map/rnsf,nsk->rfk/dot_general | solution.py:38
  121.9 10.3 %psum.28 = f32[64]{0:T(128)S(1)} all-reduce(f32[64]{0:T(128)S(1)} %fusion.7), channel_id=1, replica_groups=mesh['blk_0'=4,'blk_1'=4,'blk_2'=4,'blk_3'=2,'rep'=2] {'blk_0'}, use_global_device_ids=true, to_apply=%region_1.2 | all-reduce | flops 64 | bytes 512 | tf_op jit(solution)/shard_map/psum | solution.py:14
  132.1 8.6 %psum.29 = f32[64]{0:T(128)S(1)} all-reduce(f32[64]{0:T(128)S(1)} %psum.28), channel_id=1, replica_groups=mesh['blk_0'=4,'blk_1'=4,'blk_2'=4,'blk_3'=2,'rep'=2] {'blk_1'}, use_global_device_ids=true, to_apply=%region_2.3 | all-reduce | flops 64 | bytes 512 | tf_op jit(solution)/shard_map/psum | solution.py:14
  140.7 8.4 %psum.30 = f32[64]{0:T(128)S(1)} all-reduce(f32[64]{0:T(128)S(1)} %psum.29), channel_id=1, replica_groups=mesh['blk_0'=4,'blk_1'=4,'blk_2'=4,'blk_3'=2,'rep'=2] {'blk_2'}, use_global_device_ids=true, to_apply=%region_3.4 | all-reduce | flops 64 | bytes 512 | tf_op jit(solution)/shard_map/psum | solution.py:14
  149.1 8.5 %psum.31 = f32[64]{0:T(128)S(1)} all-reduce(f32[64]{0:T(128)S(1)} %psum.30), channel_id=1, replica_groups=mesh['blk_0'=4,'blk_1'=4,'blk_2'=4,'blk_3'=2,'rep'=2] {'blk_3'}, use_global_device_ids=true, to_apply=%region_4.5 | all-reduce | flops 64 | bytes 512 | tf_op jit(solution)/shard_map/psum | solution.py:14
  (34 shorter events, 12.5 us)
Async XLA Ops:
  44.5 23.4 %copy-start.7 = (s32[256]{0:T(256)S(1)}, s32[256]{0:T(256)}, u32[]{:S(2)}) copy-start(s32[256]{0:T(256)} %param.6) | copy-start | bytes 3076
  54.0 54.5 %all-to-all-start = ((bf16[128,2,2048]{2,1,0:T(2,128)(2,1)}), bf16[128,2,2048]{2,1,0:T(2,128)(2,1)S(1)}, u32[]{:S(2)}, u32[]{:S(2)}) async-start(bf16[128,2,2048]{2,1,0:T(2,128)(2,1)} %reshape.541), calls=%async_computation | async-start | bytes 2097152 | tf_op jit(solution)/shard_map/all_to_all | solution.py:72
  97.9 4.1 %copy-start.2 = (f32[256,1,4096]{2,0,1:T(8,128)S(1)}, f32[256,1,4096]{2,0,1:T(8,128)}, u32[]{:S(2)}) copy-start(f32[256,1,4096]{2,0,1:T(8,128)} %copy.18) | copy-start | bytes 12582916
  102.1 2.9 %copy-start.1 = (f32[256,1,4096]{2,0,1:T(8,128)S(1)}, f32[256,1,4096]{2,0,1:T(8,128)}, u32[]{:S(2)}) copy-start(f32[256,1,4096]{2,0,1:T(8,128)} %copy.17) | copy-start | bytes 12582916
  103.8 2.9 %copy-start = (f32[256,1,4096]{2,0,1:T(8,128)S(1)}, f32[256,1,4096]{2,0,1:T(8,128)}, u32[]{:S(2)}) copy-start(f32[256,1,4096]{2,0,1:T(8,128)} %copy.16) | copy-start | bytes 12582916
  109.9 1.6 %copy-start.3 = (bf16[256,1,4096]{2,0,1:T(8,128)(2,1)S(1)}, bf16[256,1,4096]{2,0,1:T(8,128)(2,1)}, u32[]{:S(2)}) copy-start(bf16[256,1,4096]{2,0,1:T(8,128)(2,1)} %multiply_convert_fusion) | copy-start | bytes 6291460
  109.9 2.2 %copy-start.4 = (bf16[256,1,4096]{2,0,1:T(8,128)(2,1)S(1)}, bf16[256,1,4096]{2,0,1:T(8,128)(2,1)}, u32[]{:S(2)}) copy-start(bf16[256,1,4096]{2,0,1:T(8,128)(2,1)} %multiply_convert_fusion.1) | copy-start | bytes 6291460
  109.9 2.8 %copy-start.5 = (bf16[256,1,4096]{2,0,1:T(8,128)(2,1)S(1)}, bf16[256,1,4096]{2,0,1:T(8,128)(2,1)}, u32[]{:S(2)}) copy-start(bf16[256,1,4096]{2,0,1:T(8,128)(2,1)} %multiply_convert_fusion.2) | copy-start | bytes 6291460
  110.0 3.4 %copy-start.6 = (bf16[256,1,4096]{2,0,1:T(8,128)(2,1)S(1)}, bf16[256,1,4096]{2,0,1:T(8,128)(2,1)}, u32[]{:S(2)}) copy-start(bf16[256,1,4096]{2,0,1:T(8,128)(2,1)} %multiply_convert_fusion.3) | copy-start | bytes 6291460
where the time goes:
time: 159 us; the launch traced here: 158 us
  local copies, waits for them, and re-layouts  63.1 us (40%)
  blocking collectives  35.8 us (23%)
  other arithmetic  29.2 us (18%)
  matrix products  14.1 us (9%)
  starting transfers between devices  13.8 us (9%)
  between operations  2.12 us (1%)
    psum x4, blocking collectives, one_axis_at_a_time(): x = lax.psum(x, axis)  35.8 us
    slice x1, local copies, waits for them, and re-layouts, shards(): legendre[pair_index]  17.4 us
    all_to_all x1, starting transfers between devices, shards(): lax.all_to_all(spectra, BLK, split_axis=0, concat_axis=1, tiled=True)  13.8 us
    add x2, local copies, waits for them, and re-layouts, basis_rows(): sin_coarse * cos_fine + cos_coarse * sin_fine  11.2 us
    sub x2, local copies, waits for them, and re-layouts, basis_rows(): cos_coarse * cos_fine - sin_coarse * sin_fine  11.2 us
    unnamed x18, local copies, waits for them, and re-layouts  10.2 us
    dot_general x1, matrix products, fourier(): jnp.einsum('rnsf,nsk->rfk', received, fourier_basis, preferred_element_ty...  7.67 us
    sub x1, other arithmetic, basis_rows(): cos_coarse * cos_fine - sin_coarse * sin_fine  6.49 us
  transfers between devices with their start and end apart: 1, of which 0 were waited for; matrix products, arithmetic and copies ran while one was open for 25% of the time, Pallas kernels for 0%

commit v1 on v0

--- a/solution.py
+++ b/solution.py
@@ -11,7 +11,8 @@
 
 def one_axis_at_a_time(x, axes):
     for axis in axes:
-        x = lax.psum(x, axis)
+        parts = lax.all_gather(x, axis, axis=0, tiled=False)
+        x = parts.sum(axis=0)
     return x
 
 

time: 159 us -> 166 us (1.044)
  local copies, waits for them, and re-layouts: 63.1 us -> 67 us
  between operations: 2.12 us -> 4.8 us
    psum x4 -> x0, blocking collectives: 35.8 us -> none  [one_axis_at_a_time(): x = lax.psum(x, axis)]
    unnamed x0 -> x4, blocking collectives: none -> 35.7 us
    unnamed x18 -> x38, local copies, waits for them, and re-layouts: 10.2 us -> 13.7 us
where the time goes in v1:
time: 166 us; the launch traced here: 165 us
  local copies, waits for them, and re-layouts  67 us (40%)
  blocking collectives  35.7 us (22%)
  other arithmetic  29.2 us (18%)
  matrix products  14.1 us (8%)
  starting transfers between devices  13.8 us (8%)
  between operations  4.8 us (3%)
    unnamed x4, blocking collectives  35.7 us
    slice x1, local copies, waits for them, and re-layouts, shards(): legendre[pair_index]  17.4 us
    all_to_all x1, starting transfers between devices, shards(): lax.all_to_all(spectra, BLK, split_axis=0, concat_axis=1, tiled=True)  13.8 us
    unnamed x38, local copies, waits for them, and re-layouts  13.7 us
    sub x2, local copies, waits for them, and re-layouts, basis_rows(): cos_coarse * cos_fine - sin_coarse * sin_fine  11.3 us
    add x2, local copies, waits for them, and re-layouts, basis_rows(): sin_coarse * cos_fine + cos_coarse * sin_fine  11.2 us
    dot_general x1, matrix products, fourier(): jnp.einsum('rnsf,nsk->rfk', received, fourier_basis, preferred_element_ty...  7.67 us
    sub x1, other arithmetic, basis_rows(): cos_coarse * cos_fine - sin_coarse * sin_fine  6.49 us
  transfers between devices with their start and end apart: 1, of which 0 were waited for; matrix products, arithmetic and copies ran while one was open for 25% of the time, Pallas kernels for 0%

profile of v1, /device:TPU:1, one launch (start us, length us, event | category | flops | bytes accessed | tf_op | source)
XLA Modules:
  0.0 164.7 jit_solution(10368791179644406463)
XLA Ops:
  4.7 3.6 %fusion.52 = (bf16[1,2049,128]{2,0,1:T(2,128)(2,1)S(1)}, bf16[1,2049,128]{2,0,1:T(2,128)(2,1)S(1)}) fusion(bf16[2,2049,128]{2,0,1:T(2,128)(2,1)} %param.4), kind=kLoop, calls=%fused_computation.100 | loop fusion | bytes 2098176 | tf_op jit(solution)/shard_map/slice | solution.py:55
  8.3 17.4 %fusion.51 = (bf16[1,2049,1024]{2,0,1:T(2,128)(2,1)S(1)}, bf16[1,2049,1024]{2,0,1:T(2,128)(2,1)}) fusion(bf16[2,2049,1024]{2,0,1:T(2,128)(2,1)} %param.5), kind=kLoop, calls=%fused_computation.99 | loop fusion | bytes 16785408 | tf_op jit(solution)/shard_map/slice | solution.py:63
  25.7 1.9 %broadcast_select_fusion.2 = (bf16[2049,128]{1,0:T(8,128)(2,1)S(1)}, bf16[2049,128]{1,0:T(8,128)(2,1)S(1)}, bf16[2049,128]{1,0:T(8,128)(2,1)S(1)}, bf16[2049,128]{1,0:T(8,128)(2,1)S(1)}) fusion(pred[2049]{0:T(1024)(128)(4,1)S(1)} %iota_compare_fusion, bf16[1,2049,128]{2,0,1:T(2,128)(2,1)S(1)} %get-tuple-element.9, ...), kind=kLoop, calls=%fused_computation.39 | loop fusion | flops 1049088 | bytes 3151362 | tf_op jit(solution)/shard_map/jit(_where)/select_n | solution.py:58
  27.7 1.5 fusion.11
  29.9 4.9 %fusion.12 = bf16[256,1024]{1,0:T(8,128)(2,1)S(1)} fusion(bf16[1,2049,1024]{2,0,1:T(2,128)(2,1)} %get-tuple-element.3, bf16[2049,128]{1,0:T(8,128)(2,1)S(1)} %get-tuple-element.7, bf16[2049,128]{1,0:T(8,128)(2,1)S(1)} %get-tuple-element.6), kind=kOutput, calls=%fused_computation.29 | convolution fusion | flops 1076626432 | bytes 5769728 | tf_op jit(solution)/shard_map/dot_general | solution.py:62
  35.6 3.1 %pad_maximum_fusion = bf16[1024,2,4,64]{3,2,1,0:T(4,128)(2,1)} fusion(bf16[1024,1,4,64]{3,2,1,0:T(4,128)(2,1)S(1)} %copy.26, bf16[1024,1,4,64]{3,2,1,0:T(4,128)(2,1)S(1)} %copy.25), kind=kLoop, calls=%fused_computation.24 | loop fusion | flops 524288 | bytes 2097152 | tf_op jit(solution)/shard_map/stack | solution.py:69
  38.6 5.8 %gather_fusion = bf16[1024,2,4,64]{3,2,1,0:T(4,128)(2,1)S(1)} fusion(bf16[1024,2,4,64]{3,2,1,0:T(4,128)(2,1)} %pad_maximum_fusion, s32[1024]{0:T(1024)S(1)} %fusion.45), kind=kCustom, calls=%fused_computation | custom fusion | bytes 2101248 | tf_op jit(solution)/shard_map/jit(_take)/gather | solution.py:70
  44.5 4.5 %broadcast_select_fusion = bf16[1024,2,4,64]{3,2,1,0:T(4,128)(2,1)} fusion(bf16[1024,2,4,64]{3,2,1,0:T(4,128)(2,1)S(1)} %gather_fusion, pred[1024]{0:T(1024)(128)(4,1)S(1)} %compare_and_fusion), kind=kLoop, calls=%fused_computation.27 | loop fusion | flops 524288 | bytes 2098176 | tf_op jit(solution)/shard_map/jit(_take)/select_n | solution.py:70
  48.9 5.1 %reshape.565 = bf16[128,2,2048]{2,1,0:T(2,128)(2,1)} reshape(bf16[1024,2,4,64]{3,2,1,0:T(4,128)(2,1)} %broadcast_select_fusion) | data formatting | bytes 2097152
  54.1 13.8 %all-to-all-start = ((bf16[128,2,2048]{2,1,0:T(2,128)(2,1)}), bf16[128,2,2048]{2,1,0:T(2,128)(2,1)S(1)}, u32[]{:S(2)}, u32[]{:S(2)}) async-start(bf16[128,2,2048]{2,1,0:T(2,128)(2,1)} %reshape.565), calls=%async_computation | async-start | bytes 2097152 | tf_op jit(solution)/shard_map/all_to_all | solution.py:73
  69.0 6.5 %multiply_subtract_fusion = (f32[256,64,64]{0,2,1:T(8,128)}, f32[256,64,64]{0,2,1:T(8,128)}, f32[256,64,64]{0,2,1:T(8,128)}, f32[256,64,64]{0,2,1:T(8,128)}) fusion(f32[256,64]{0,1:T(8,128)S(1)} %get-tuple-element.29, f32[256,64]{0,1:T(8,128)S(1)} %get-tuple-element.30, f32[256,64]{0,1:T(8,128)S(1)} %get-tuple-element.28, ...), kind=kLoop, calls=%fused_computation.19 | loop fusion | flops 12582912 | bytes 17301504 | tf_op jit(solution)/shard_map/sub | solution.py:29
  75.5 5.6 %copy.32 = f32[256,1,4096]{2,0,1:T(8,128)} copy(f32[256,1,4096]{0,2,1:T(8,128)} %bitcast.58) | data formatting | bytes 8388608 | tf_op jit(solution)/shard_map/add | solution.py:30
  81.1 5.6 %copy.31 = f32[256,1,4096]{2,0,1:T(8,128)} copy(f32[256,1,4096]{0,2,1:T(8,128)} %bitcast.57) | data formatting | bytes 8388608 | tf_op jit(solution)/shard_map/sub | solution.py:29
  86.7 5.6 %copy.30 = f32[256,1,4096]{2,0,1:T(8,128)} copy(f32[256,1,4096]{0,2,1:T(8,128)} %bitcast.56) | data formatting | bytes 8388608 | tf_op jit(solution)/shard_map/add | solution.py:30
  92.3 5.7 %copy.29 = f32[256,1,4096]{2,0,1:T(8,128)} copy(f32[256,1,4096]{0,2,1:T(8,128)} %bitcast.55) | data formatting | bytes 8388608 | tf_op jit(solution)/shard_map/sub | solution.py:29
  103.2 4.0 %multiply_convert_fusion = bf16[256,1,4096]{2,0,1:T(8,128)(2,1)} fusion(f32[256,1,4096]{2,0,1:T(8,128)} %copy.32, f32[256]{0:T(256)S(1)} %get-tuple-element.19), kind=kLoop, calls=%fused_computation.16 | loop fusion | flops 2097152 | bytes 6292480 | tf_op jit(solution)/shard_map/convert_element_type | solution.py:32
  107.2 1.8 %multiply_convert_fusion.1 = bf16[256,1,4096]{2,0,1:T(8,128)(2,1)} fusion(f32[256,1,4096]{2,0,1:T(8,128)S(1)} %copy-done.2, f32[256]{0:T(256)S(1)} %get-tuple-element.21), kind=kLoop, calls=%fused_computation.18 | loop fusion | flops 2097152 | bytes 6292480 | tf_op jit(solution)/shard_map/convert_element_type | solution.py:32
  110.2 1.8 %multiply_convert_fusion.2 = bf16[256,1,4096]{2,0,1:T(8,128)(2,1)} fusion(f32[256,1,4096]{2,0,1:T(8,128)S(1)} %copy-done.1, f32[256]{0:T(256)S(1)} %get-tuple-element.20), kind=kLoop, calls=%fused_computation.20 | loop fusion | flops 2097152 | bytes 6292480 | tf_op jit(solution)/shard_map/convert_element_type | solution.py:32
  112.0 1.8 %multiply_convert_fusion.3 = bf16[256,1,4096]{2,0,1:T(8,128)(2,1)} fusion(f32[256,1,4096]{2,0,1:T(8,128)S(1)} %copy-done, f32[256]{0:T(256)S(1)} %get-tuple-element.18), kind=kLoop, calls=%fused_computation.22 | loop fusion | flops 2097152 | bytes 6292480 | tf_op jit(solution)/shard_map/convert_element_type | solution.py:32
  118.6 7.7 %bitcast_convert_fusion = (bf16[8,64,4096]{2,1,0:T(8,128)(2,1)}, f32[8,64,4096,1]{2,1,3,0:T(8,128)S(1)}) fusion(bf16[256,1,4096]{2,0,1:T(8,128)(2,1)S(1)} %copy-done.3, bf16[256,1,4096]{2,0,1:T(8,128)(2,1)S(1)} %copy-done.4, bf16[256,1,4096]{2,0,1:T(8,128)(2,1)S(1)} %copy-done.5, bf16[256,1,4096]{2,0,1:T(8,128)(2,1)S(1)} %copy-done.6, ...), kind=kOutput, calls=%fused_computation.10 | convolution fusion | flops 4309647360 | bytes 22020096 | tf_op jit(solution)/shard_map/rnsf,nsk->rfk/dot_general | solution.py:39
  127.3 10.3 %all-reduce = f32[256]{0:T(256)S(1)} all-reduce(f32[256]{0:T(256)S(1)} %dynamic-update-slice), channel_id=2, replica_groups=mesh['blk_0'=4,'blk_1'=4,'blk_2'=4,'blk_3'=2,'rep'=2] {'blk_0'}, use_global_device_ids=true, to_apply=%add | all-reduce | flops 256 | bytes 2048
  137.9 8.5 %all-reduce.1 = f32[256]{0:T(256)S(1)} all-reduce(f32[256]{0:T(256)S(1)} %dynamic-update-slice.1), channel_id=3, replica_groups=mesh['blk_0'=4,'blk_1'=4,'blk_2'=4,'blk_3'=2,'rep'=2] {'blk_1'}, use_global_device_ids=true, to_apply=%add.1 | all-reduce | flops 256 | bytes 2048
  146.8 8.4 %all-reduce.2 = f32[256]{0:T(256)S(1)} all-reduce(f32[256]{0:T(256)S(1)} %dynamic-update-slice.2), channel_id=4, replica_groups=mesh['blk_0'=4,'blk_1'=4,'blk_2'=4,'blk_3'=2,'rep'=2] {'blk_2'}, use_global_device_ids=true, to_apply=%add.2 | all-reduce | flops 256 | bytes 2048
  155.5 8.5 %all-reduce.3 = f32[128]{0:T(128)S(1)} all-reduce(f32[128]{0:T(128)S(1)} %dynamic-update-slice.3), channel_id=5, replica_groups=mesh['blk_0'=4,'blk_1'=4,'blk_2'=4,'blk_3'=2,'rep'=2] {'blk_3'}, use_global_device_ids=true, to_apply=%add.3 | all-reduce | flops 128 | bytes 1024
  (62 shorter events, 16.4 us)
Async XLA Ops:
  44.4 23.4 %copy-start.7 = (s32[256]{0:T(256)S(1)}, s32[256]{0:T(256)}, u32[]{:S(2)}) copy-start(s32[256]{0:T(256)} %param.6) | copy-start | bytes 3076
  54.1 59.6 %all-to-all-start = ((bf16[128,2,2048]{2,1,0:T(2,128)(2,1)}), bf16[128,2,2048]{2,1,0:T(2,128)(2,1)S(1)}, u32[]{:S(2)}, u32[]{:S(2)}) async-start(bf16[128,2,2048]{2,1,0:T(2,128)(2,1)} %reshape.565), calls=%async_computation | async-start | bytes 2097152 | tf_op jit(solution)/shard_map/all_to_all | solution.py:73
  92.3 5.7 %copy-start.11 = (u32[256]{0:T(256)S(1)}, u32[256]{0:T(256)}, u32[]{:S(2)}) copy-start(u32[256]{0:T(256)} %constant.97) | copy-start | bytes 3076
  92.3 6.3 %copy-start.10 = (u32[256]{0:T(256)S(1)}, u32[256]{0:T(256)}, u32[]{:S(2)}) copy-start(u32[256]{0:T(256)} %constant.102) | copy-start | bytes 3076
  92.3 8.3 %copy-start.9 = (u32[256]{0:T(256)S(1)}, u32[256]{0:T(256)}, u32[]{:S(2)}) copy-start(u32[256]{0:T(256)} %constant.107) | copy-start | bytes 3076
  92.3 9.6 %copy-start.8 = (u32[256]{0:T(256)S(1)}, u32[256]{0:T(256)}, u32[]{:S(2)}) copy-start(u32[256]{0:T(256)} %constant.112) | copy-start | bytes 3076
  98.0 9.2 %copy-start.2 = (f32[256,1,4096]{2,0,1:T(8,128)S(1)}, f32[256,1,4096]{2,0,1:T(8,128)}, u32[]{:S(2)}) copy-start(f32[256,1,4096]{2,0,1:T(8,128)} %copy.31) | copy-start | bytes 12582916
  107.2 2.9 %copy-start.1 = (f32[256,1,4096]{2,0,1:T(8,128)S(1)}, f32[256,1,4096]{2,0,1:T(8,128)}, u32[]{:S(2)}) copy-start(f32[256,1,4096]{2,0,1:T(8,128)} %copy.30) | copy-start | bytes 12582916
  109.0 2.9 %copy-start = (f32[256,1,4096]{2,0,1:T(8,128)S(1)}, f32[256,1,4096]{2,0,1:T(8,128)}, u32[]{:S(2)}) copy-start(f32[256,1,4096]{2,0,1:T(8,128)} %copy.29) | copy-start | bytes 12582916
  115.1 1.6 copy-start.3
  115.1 2.2 %copy-start.4 = (bf16[256,1,4096]{2,0,1:T(8,128)(2,1)S(1)}, bf16[256,1,4096]{2,0,1:T(8,128)(2,1)}, u32[]{:S(2)}) copy-start(bf16[256,1,4096]{2,0,1:T(8,128)(2,1)} %multiply_convert_fusion.1) | copy-start | bytes 6291460
  115.1 2.8 %copy-start.5 = (bf16[256,1,4096]{2,0,1:T(8,128)(2,1)S(1)}, bf16[256,1,4096]{2,0,1:T(8,128)(2,1)}, u32[]{:S(2)}) copy-start(bf16[256,1,4096]{2,0,1:T(8,128)(2,1)} %multiply_convert_fusion.2) | copy-start | bytes 6291460
  115.1 3.4 %copy-start.6 = (bf16[256,1,4096]{2,0,1:T(8,128)(2,1)S(1)}, bf16[256,1,4096]{2,0,1:T(8,128)(2,1)}, u32[]{:S(2)}) copy-start(bf16[256,1,4096]{2,0,1:T(8,128)(2,1)} %multiply_convert_fusion.3) | copy-start | bytes 6291460
